TPU v7x, 32 devices: a whole 2x2x4 slice. The times are simulated.
32 devices in a mesh: dp: 8 (over y, x, core), head: 4 (over z).
Axes of the slice: x: 2, y: 2, z: 4, core: 2. Of those that a mesh axis runs over, the one named last changes fastest.
Arguments:
- attn_queries: bfloat16 [4096, 1536], P('dp', 'head'), may hold values from -64 to 64
- keys: bfloat16 [4096, 256], P('dp'), may hold values from -6 to 6
- values: bfloat16 [4096, 256], P('dp'), may hold values from -6 to 6
- out_weight: bfloat16 [1536, 1536], P('head'), may hold values from -0.15625 to 0.15625
- lengths: int32 [8, 8], P('dp'), may hold values from 1 to 256, 512 in all within a row
- queries: bfloat16 [32, 1536], P('dp', 'head'), may hold values from -48 to 48
- positives: int32 [32], replicated, may hold values from 0 to 63
Outputs:
- d_values: bfloat16 [4096, 256], P('dp', 'head')
- loss: float32 [], replicated
Inputs may be any that keep to these rules, and one draw needn't show every extreme that they name: `lengths`: each row sums to 512.
All inputs are finite; a program needn't handle non-finite values.
Results may differ from a plain program's by a relative error of at most 0.0072.
Values may be sent and summed in bfloat16 or wider, within the bound.
A program may use at most 64 MiB of HBM per device.

v0:
```python
import functools
import math

import jax
import jax.numpy as jnp
from jax import lax
from jax.experimental import pallas as pl
from jax.experimental.pallas import tpu as pltpu
from jax.sharding import PartitionSpec as P

HEADS = 12
KV_HEADS = 2
HD = 128
LANES = 128
SUBLANES = 8

sim_scale = 20.0
loss_scale = 32768.0

NT = (((1,), (1,)), ((), ()))
NN = (((1,), (0,)), ((), ()))
f32 = jnp.float32
bf16 = jnp.bfloat16


def mm(a, b, dims):
    return lax.dot_general(a, b, dims, preferred_element_type=f32)


def hi_lo(x):
    hi = x.astype(bf16)
    return hi, (x - hi.astype(f32)).astype(bf16)


def each(first, last, body):
    if last - first <= 8:
        for k in range(first, last):
            body(k)
    else:
        lax.fori_loop(first, last, lambda k, c: (body(k), c)[1], 0)


def fold(last, body, carry):
    if last <= 8:
        for k in range(last):
            carry = body(k, carry)
        return carry
    return lax.fori_loop(0, last, body, carry)


def remote(src, dst, send, recv, axis, peer):
    return pltpu.make_async_remote_copy(
        src_ref=src, dst_ref=dst, send_sem=send, recv_sem=recv,
        device_id={axis: peer}, device_id_type=pl.DeviceIdType.MESH,
    )


def kernel(
    n_dp, n_head,
    lens_hbm, pos_hbm, q_hbm, k_hbm, v_hbm, w_hbm, qry_hbm,
    out_ref, loss_ref,
    lens, pos_ref, q_v, k_v, v_v, w_v, qall, qf, c_own, c_in, emb_slot, stat, qw_own, qw_in, uw_own, uw_in,
    a_ref, load_sem, qload_sem, q1_send, q1_recv, q2_send, q2_recv, e_send, e_recv, s_send, s_recv,
    p_send, p_recv,
):
    dp = lax.axis_index("dp")
    head = lax.axis_index("head")
    partner = head + 1 - 2 * lax.rem(head, 2)
    seq, width = q_v.shape
    heads = width // HD
    group = HEADS // KV_HEADS
    docs = lens.shape[1]
    rows = qall.shape[2]
    nq = n_dp * rows
    kv_cols = pl.ds(pl.multiple_of((head * heads // group) * HD, HD), HD)
    blocks = seq // LANES

    k_load = pltpu.make_async_copy(k_hbm.at[:, kv_cols], k_v, load_sem.at[0])
    v_load = pltpu.make_async_copy(v_hbm.at[:, kv_cols], v_v, load_sem.at[1])
    w_load = pltpu.make_async_copy(w_hbm, w_v, load_sem.at[2])
    qry_load = pltpu.make_async_copy(qry_hbm, qall.at[dp, head], load_sem.at[3])
    q_loads = [
        pltpu.make_async_copy(
            q_hbm.at[pl.ds(b * LANES, LANES)], q_v.at[pl.ds(b * LANES, LANES)], qload_sem.at[b]
        )
        for b in range(blocks)
    ]
    lens_load = pltpu.make_async_copy(lens_hbm, lens, load_sem.at[4])
    pos_load = pltpu.make_async_copy(pos_hbm, pos_ref, load_sem.at[5])
    lens_load.start()
    k_load.start()
    for load in q_loads:
        load.start()
    qry_load.start()
    v_load.start()
    w_load.start()
    pos_load.start()

    barrier = pltpu.get_barrier_semaphore()

    def peer(me, k, n):
        return lax.bitwise_xor(me, n - k)

    def greet(axis, me, n):
        def one(k):
            pl.semaphore_signal(
                barrier, inc=1, device_id={axis: peer(me, k, n)}, device_id_type=pl.DeviceIdType.MESH
            )
        each(1, n, one)

    greet("head", head, n_head)
    greet("dp", dp, n_dp)

    def q1(k, owner):
        slot = qall.at[dp, owner]
        return remote(slot, slot, q1_send.at[k], q1_recv.at[k], "head", peer(head, k, n_head))

    def q2(x, k, owner):
        slot = qall.at[owner, lax.bitwise_xor(head, x)]
        return remote(slot, slot, q2_send.at[x, k], q2_recv.at[x, k], "dp", peer(dp, k, n_dp))

    def e_copy(k, owner):
        slot = emb_slot.at[owner]
        return remote(slot, slot, e_send.at[k], e_recv.at[k], "head", peer(head, k, n_head))

    def s_copy(k, owner):
        slot = stat.at[owner]
        return remote(slot, slot, s_send.at[k], s_recv.at[k], "dp", peer(dp, k, n_dp))

    ii = lax.broadcasted_iota(jnp.int32, (1, seq), 1)
    drow = lax.broadcasted_iota(jnp.int32, (docs, 1), 0)
    start_row = jnp.zeros((1, seq), jnp.int32)
    starts = jnp.zeros((docs, 1), jnp.int32)
    lens_col = jnp.zeros((docs, 1), jnp.int32)
    begin = jnp.int32(0)
    lens_load.wait()
    for d in range(docs):
        start_row = jnp.where(ii >= begin, begin, start_row)
        starts = jnp.where(drow == d, begin, starts)
        lens_col = jnp.where(drow == d, lens[0, d], lens_col)
        begin = begin + lens[0, d]
    len_f = lens_col.astype(f32)
    member = (ii >= starts) & (ii < starts + lens_col)

    k_load.wait()
    ones = jnp.ones((docs, LANES), bf16)
    rate = math.log2(math.e) / math.sqrt(HD)
    sums = [[None] * blocks for _ in range(heads)]
    for b in range(blocks):
        q_loads[b].wait()
        n = (b + 1) * LANES
        cols = slice(b * LANES, n)
        jj = lax.broadcasted_iota(jnp.int32, (n, LANES), 0)
        allowed = (jj >= start_row[:, cols]) & (jj <= ii[:, cols])
        keys = k_v[:n, :]
        for h in range(heads):
            s = mm(keys, q_v[cols, h * HD:(h + 1) * HD], NT)
            s = jnp.where(allowed, s, -1e30)
            e = jnp.exp2((s - jnp.max(s, axis=0, keepdims=True)) * rate)
            p = (e * (1.0 / jnp.sum(e, axis=0, keepdims=True))).astype(bf16)
            part = mm(ones, p, NT)
            for j in range(b + 1):
                piece = part[:, j * LANES:(j + 1) * LANES]
                sums[h][j] = piece if sums[h][j] is None else sums[h][j] + piece

    csum = [jnp.concatenate(sums[h], axis=1) for h in range(heads)]
    spread = jnp.concatenate([jnp.where(member, csum[h], 0.0) for h in range(heads)], axis=0)
    s_hi, s_lo = hi_lo(spread)
    v_load.wait()
    span = heads * docs
    pooled = mm(jnp.concatenate([s_hi, s_lo], axis=0), v_v[...], NN)
    pooled = pooled[:span] + pooled[span:]
    pooled = jnp.concatenate(
        [pooled[h * docs:(h + 1) * docs] for h in range(heads)], axis=1
    ) / len_f
    p_hi, p_lo = hi_lo(pooled)
    w_load.wait()
    emb = mm(jnp.concatenate([p_hi, p_lo], axis=0), w_v[...], NN)
    emb_slot[head] = (emb[:docs] + emb[docs:]).astype(bf16)

    qry_load.wait()
    pl.semaphore_wait(barrier, n_head - 1 + n_dp - 1)
    each(1, n_head, lambda k: q1(k, head).start())
    each(1, n_dp, lambda k: q2(0, k, dp).start())
    each(1, n_head, lambda k: e_copy(k, head).start())

    rid = lax.broadcasted_iota(jnp.int32, (docs, 1), 0)
    packed = jnp.zeros((docs, seq), f32)
    for h in range(heads):
        packed = jnp.where(rid == h, csum[h], packed)
    c_own[...] = packed
    c_copy = remote(c_own, c_in, p_send.at[0], p_recv.at[0], "head", partner)
    c_copy.start()
    for x in range(1, n_head):
        q1(n_head - x, lax.bitwise_xor(head, x)).wait_recv()
        each(1, n_dp, lambda k: q2(x, k, dp).start())

    c_copy.wait_recv()
    other = jnp.concatenate(
        [jnp.where(member, c_in[h:h + 1, :], 0.0) for h in range(heads)], axis=0
    )
    both = jnp.concatenate([spread, other], axis=0)
    b_hi, b_lo = hi_lo(both)
    a_ref[...] = jnp.concatenate([b_hi, b_lo], axis=0)

    each(1, n_head, lambda k: e_copy(k, peer(head, k, n_head)).wait_recv())
    emb = emb_slot[0].astype(f32)
    for o in range(1, n_head):
        emb = emb + emb_slot[o].astype(f32)
    rnorm = 1.0 / jnp.sqrt(jnp.sum(emb * emb, axis=1, keepdims=True) + 1e-06)
    unit = emb * rnorm
    u_hi, u_lo = hi_lo(unit)
    u_both = jnp.concatenate([u_hi, u_lo], axis=0)
    for x in range(n_head):
        each(1, n_dp, lambda k: q2(x, k, peer(dp, k, n_dp)).wait_recv())
    pack = max(1, SUBLANES // rows)

    def assemble(t):
        for o in range(n_head):
            piece = jnp.concatenate([qall[t * pack + u, o].astype(f32) for u in range(pack)], axis=0)
            qf[pl.ds(t * pack * rows, pack * rows), o * width:(o + 1) * width] = piece

    each(0, n_dp // pack, assemble)
    qmat = qf[...].astype(bf16)
    sims = sim_scale * mm(u_both, qmat, NT)
    logits = sims[:docs]
    full = logits + sims[docs:]
    pos_load.wait()
    chosen = (pos_ref[...] == dp * docs + drow).astype(f32)
    top = jnp.max(logits, axis=0, keepdims=True)
    total = jnp.sum(jnp.exp(logits - top), axis=0, keepdims=True)
    hit = jnp.sum(logits * chosen, axis=0, keepdims=True)
    srow = lax.broadcasted_iota(jnp.int32, (stat.shape[1], 1), 0)
    stat[dp] = jnp.where(srow == 0, top, jnp.where(srow == 1, total, hit))
    each(1, n_dp, lambda k: s_copy(k, dp).start())

    qw_own[...] = mm(qmat, w_v[...], NT).astype(bf16)
    qw_copy = remote(qw_own, qw_in, p_send.at[1], p_recv.at[1], "head", partner)
    qw_copy.start()
    uw = mm(u_both, w_v[...], NT)
    uw = uw[:docs] + uw[docs:]
    uw_own[...] = uw
    uw_copy = remote(uw_own, uw_in, p_send.at[2], p_recv.at[2], "head", partner)
    uw_copy.start()

    qw_copy.wait_recv()
    qw = jnp.concatenate([qw_own[...], qw_in[...]], axis=1)
    qw2 = jnp.concatenate([qw, qw], axis=0)
    factor = rnorm * (loss_scale / len_f)

    each(1, n_dp, lambda k: s_copy(k, peer(dp, k, n_dp)).wait_recv())
    top = fold(
        n_dp, lambda k, c: jnp.maximum(c, stat[k][0:1]), jnp.full((1, nq), -jnp.inf, f32)
    )

    def gather(k, c):
        tile = stat[k]
        return c[0] + tile[1:2] * jnp.exp(tile[0:1] - top), c[1] + tile[2:3]

    zero = jnp.zeros((1, nq), f32)
    total, hit = fold(n_dp, gather, (zero, zero))
    lse = top + jnp.log(total)
    loss_ref[0, 0] = jnp.sum(lse - hit) * (1.0 / nq)
    dl = jnp.exp(logits - lse) - chosen
    inner = jnp.sum(dl * full, axis=1, keepdims=True)
    d_hi, d_lo = hi_lo(dl)
    g = sim_scale * mm(jnp.concatenate([d_hi, d_lo], axis=1), qw2, NN)
    uw_copy.wait_recv()
    uw2 = jnp.concatenate([uw, uw_in[...]], axis=1)
    g = factor * (g - inner * uw2)
    small = jnp.concatenate(
        [g[:, h * HD:(h + 1) * HD] for h in range(2 * heads)], axis=0
    )
    small = jnp.concatenate([small, small], axis=0).T
    half = HD // 2
    small = jnp.where(lax.rem(head, 2) == 0, small[:half], small[half:]).astype(bf16)
    out_ref[...] = mm(small, a_ref[...], NN).astype(bf16)

    each(1, n_head, lambda k: q1(k, head).wait_send())
    for x in range(n_head):
        each(1, n_dp, lambda k: q2(x, k, dp).wait_send())
    each(1, n_head, lambda k: e_copy(k, head).wait_send())
    each(1, n_dp, lambda k: s_copy(k, dp).wait_send())
    c_copy.wait_send()
    qw_copy.wait_send()
    uw_copy.wait_send()


def per_device(n_dp, n_head, attn_queries, keys, values, out_weight, lengths, queries, positives):
    seq, width = attn_queries.shape
    heads = width // HD
    docs = lengths.shape[1]
    rows = queries.shape[0]
    nq = n_dp * rows
    model = out_weight.shape[1]
    blocks = seq // LANES
    dma = pltpu.SemaphoreType.DMA
    hbm = pl.BlockSpec(memory_space=pltpu.HBM)
    vmem = pl.BlockSpec(memory_space=pltpu.VMEM)
    smem = pl.BlockSpec(memory_space=pltpu.SMEM)
    d_values, loss = pl.pallas_call(
        functools.partial(kernel, n_dp, n_head),
        out_shape=(
            jax.ShapeDtypeStruct((HD // 2, seq), bf16),
            jax.ShapeDtypeStruct((1, 1), f32),
        ),
        in_specs=[hbm, hbm, hbm, hbm, hbm, hbm, hbm],
        out_specs=(vmem, smem),
        scratch_shapes=[
            pltpu.SMEM((1, docs), jnp.int32),
            pltpu.VMEM((1, nq), jnp.int32),
            pltpu.VMEM((seq, width), bf16),
            pltpu.VMEM((seq, HD), bf16),
            pltpu.VMEM((seq, HD), bf16),
            pltpu.VMEM((width, model), bf16),
            pltpu.VMEM((n_dp, n_head, rows, width), bf16),
            pltpu.VMEM((nq, model), f32),
            pltpu.VMEM((docs, seq), f32),
            pltpu.VMEM((docs, seq), f32),
            pltpu.VMEM((n_head, docs, model), bf16),
            pltpu.VMEM((n_dp, SUBLANES // 2, nq), f32),
            pltpu.VMEM((nq, width), bf16),
            pltpu.VMEM((nq, width), bf16),
            pltpu.VMEM((docs, width), f32),
            pltpu.VMEM((docs, width), f32),
            pltpu.VMEM((4 * heads * docs, seq), bf16),
            dma((6,)),
            dma((blocks,)),
            dma((n_head,)),
            dma((n_head,)),
            dma((n_head, n_dp)),
            dma((n_head, n_dp)),
            dma((n_head,)),
            dma((n_head,)),
            dma((n_dp,)),
            dma((n_dp,)),
            dma((3,)),
            dma((3,)),
        ],
        compiler_params=pltpu.CompilerParams(collective_id=0, has_side_effects=True),
    )(lengths, positives.reshape(1, nq), attn_queries, keys, values, out_weight, queries)
    return d_values.T, loss.reshape(())


def solution(mesh):
    placed = (
        P("dp", "head"),
        P("dp", None),
        P("dp", None),
        P("head", None),
        P("dp", None),
        P("dp", "head"),
        P(),
    )
    return jax.shard_map(
        functools.partial(per_device, mesh.shape["dp"], mesh.shape["head"]),
        mesh=mesh, in_specs=placed, out_specs=(P("dp", "head"), P()), check_vma=False,
    )
```

profile of v0, /device:TPU:0, one launch (start us, length us, event | category | flops | bytes accessed | tf_op | source)
XLA Modules:
  0.0 24.4 jit_solution(30784377362072720)
XLA Ops:
  0.6 20.5 %shard_map.86 = (bf16[64,512]{1,0:T(8,128)(2,1)}, f32[1,1]{1,0:T(1,128)}) custom-call(s32[1,8]{1,0:T(1,128)} %lens_hbm.1, s32[1,32]{1,0:T(1,128)} %bitcast.4, bf16[512,384]{1,0:T(8,128)(2,1)} %q_hbm.1, bf16[512,256]{1,0:T(8,128)(2,1)} %k_hbm.1, bf16[512,256]{1,0:T(8,128)(2,1)} %v_hbm.1, bf16[384,1536]{1,0:T(8,128)(2,1)} %w_hbm.1, bf16[4,384]{1,0:T(4,128)(2,1)} %qry_hbm.1), custom_call_target="tpu_custom_call" | custom-call | tf_op jit(solution)/shard_map/pallas_call | solution.py:301
  21.1 1.5 %copy.11 = bf16[512,64]{0,1:T(8,128)(2,1)} copy(bf16[512,64]{0,1:T(8,128)(2,1)} %bitcast.3) | data formatting | bytes 131072
where the time goes:
time: 24.6 us; the launch traced here: 24.4 us
  Pallas kernels  20.5 us (83%)
  between operations  2.39 us (10%)
  local copies, waits for them, and re-layouts  1.47 us (6%)
    pallas_call x1, Pallas kernels, per_device(): pl.pallas_call(functools.partial(kernel, n_dp, n_head), out_shape=(jax.Sh...  20.5 us
    unnamed x1, local copies, waits for them, and re-layouts  1.47 us

commit v1 on v0

--- a/solution.py
+++ b/solution.py
@@ -53,6 +53,10 @@
         src_ref=src, dst_ref=dst, send_sem=send, recv_sem=recv,
         device_id={axis: peer}, device_id_type=pl.DeviceIdType.MESH,
     )
+
+
+def wait_all(ref, sem):
+    pltpu.make_async_copy(ref, ref, sem).wait()
 
 
 def kernel(
@@ -65,9 +69,11 @@
 ):
     dp = lax.axis_index("dp")
     head = lax.axis_index("head")
-    partner = head + 1 - 2 * lax.rem(head, 2)
+    side = lax.rem(head, 2)
+    partner = head + 1 - 2 * side
     seq, width = q_v.shape
     heads = width // HD
+    half = HD // 2
     group = HEADS // KV_HEADS
     docs = lens.shape[1]
     rows = qall.shape[2]
@@ -89,9 +95,10 @@
     pos_load = pltpu.make_async_copy(pos_hbm, pos_ref, load_sem.at[5])
     lens_load.start()
     k_load.start()
-    for load in q_loads:
+    q_loads[0].start()
+    qry_load.start()
+    for load in q_loads[1:]:
         load.start()
-    qry_load.start()
     v_load.start()
     w_load.start()
     pos_load.start()
@@ -113,19 +120,19 @@
 
     def q1(k, owner):
         slot = qall.at[dp, owner]
-        return remote(slot, slot, q1_send.at[k], q1_recv.at[k], "head", peer(head, k, n_head))
+        return remote(slot, slot, q1_send, q1_recv.at[k], "head", peer(head, k, n_head))
 
     def q2(x, k, owner):
         slot = qall.at[owner, lax.bitwise_xor(head, x)]
-        return remote(slot, slot, q2_send.at[x, k], q2_recv.at[x, k], "dp", peer(dp, k, n_dp))
+        return remote(slot, slot, q2_send, q2_recv.at[x], "dp", peer(dp, k, n_dp))
 
     def e_copy(k, owner):
         slot = emb_slot.at[owner]
-        return remote(slot, slot, e_send.at[k], e_recv.at[k], "head", peer(head, k, n_head))
+        return remote(slot, slot, e_send, e_recv, "head", peer(head, k, n_head))
 
     def s_copy(k, owner):
         slot = stat.at[owner]
-        return remote(slot, slot, s_send.at[k], s_recv.at[k], "dp", peer(dp, k, n_dp))
+        return remote(slot, slot, s_send, s_recv, "dp", peer(dp, k, n_dp))
 
     ii = lax.broadcasted_iota(jnp.int32, (1, seq), 1)
     drow = lax.broadcasted_iota(jnp.int32, (docs, 1), 0)
@@ -162,6 +169,11 @@
             for j in range(b + 1):
                 piece = part[:, j * LANES:(j + 1) * LANES]
                 sums[h][j] = piece if sums[h][j] is None else sums[h][j] + piece
+        if b == 1:
+            qry_load.wait()
+            pl.semaphore_wait(barrier, n_head - 1 + n_dp - 1)
+            each(1, n_head, lambda k: q1(k, head).start())
+            each(1, n_dp, lambda k: q2(0, k, dp).start())
 
     csum = [jnp.concatenate(sums[h], axis=1) for h in range(heads)]
     spread = jnp.concatenate([jnp.where(member, csum[h], 0.0) for h in range(heads)], axis=0)
@@ -177,17 +189,12 @@
     w_load.wait()
     emb = mm(jnp.concatenate([p_hi, p_lo], axis=0), w_v[...], NN)
     emb_slot[head] = (emb[:docs] + emb[docs:]).astype(bf16)
-
-    qry_load.wait()
-    pl.semaphore_wait(barrier, n_head - 1 + n_dp - 1)
-    each(1, n_head, lambda k: q1(k, head).start())
-    each(1, n_dp, lambda k: q2(0, k, dp).start())
     each(1, n_head, lambda k: e_copy(k, head).start())
 
-    rid = lax.broadcasted_iota(jnp.int32, (docs, 1), 0)
-    packed = jnp.zeros((docs, seq), f32)
+    rid = lax.broadcasted_iota(jnp.int32, (c_own.shape[0], 1), 0)
+    packed = jnp.zeros(c_own.shape, f32)
     for h in range(heads):
-        packed = jnp.where(rid == h, csum[h], packed)
+        packed = jnp.where(rid == h, csum[h][:c_own.shape[0]], packed)
     c_own[...] = packed
     c_copy = remote(c_own, c_in, p_send.at[0], p_recv.at[0], "head", partner)
     c_copy.start()
@@ -195,6 +202,28 @@
         q1(n_head - x, lax.bitwise_xor(head, x)).wait_recv()
         each(1, n_dp, lambda k: q2(x, k, dp).start())
 
+    for x in range(n_head):
+        wait_all(qall.at[pl.ds(0, n_dp - 1), 0], q2_recv.at[x])
+    pack = max(1, SUBLANES // rows)
+
+    def assemble(t):
+        for o in range(n_head):
+            piece = jnp.concatenate([qall[t * pack + u, o].astype(f32) for u in range(pack)], axis=0)
+            qf[pl.ds(t * pack * rows, pack * rows), o * width:(o + 1) * width] = piece
+
+    each(0, n_dp // pack, assemble)
+    qmat = qf[...].astype(bf16)
+
+    def w_half(which):
+        return jnp.concatenate(
+            [w_v[pl.ds(pl.multiple_of(h * HD + which * half, half), half), :] for h in range(heads)], axis=0
+        )
+
+    qw_own[...] = mm(qmat, w_half(1 - side), NT).astype(bf16)
+    qw_copy = remote(qw_own, qw_in, p_send.at[1], p_recv.at[1], "head", partner)
+    qw_copy.start()
+    qw_mine = mm(qmat, w_half(side), NT).astype(bf16)
+
     c_copy.wait_recv()
     other = jnp.concatenate(
         [jnp.where(member, c_in[h:h + 1, :], 0.0) for h in range(heads)], axis=0
@@ -202,8 +231,13 @@
     both = jnp.concatenate([spread, other], axis=0)
     b_hi, b_lo = hi_lo(both)
     a_ref[...] = jnp.concatenate([b_hi, b_lo], axis=0)
-
-    each(1, n_head, lambda k: e_copy(k, peer(head, k, n_head)).wait_recv())
+    qw_copy.wait_recv()
+    qw = jnp.concatenate([qw_mine, qw_in[...]], axis=1)
+    qw2 = jnp.concatenate([qw, qw], axis=0)
+    pos_load.wait()
+    chosen = (pos_ref[...] == dp * docs + drow).astype(f32)
+
+    wait_all(emb_slot.at[pl.ds(0, n_head - 1)], e_recv)
     emb = emb_slot[0].astype(f32)
     for o in range(1, n_head):
         emb = emb + emb_slot[o].astype(f32)
@@ -211,22 +245,9 @@
     unit = emb * rnorm
     u_hi, u_lo = hi_lo(unit)
     u_both = jnp.concatenate([u_hi, u_lo], axis=0)
-    for x in range(n_head):
-        each(1, n_dp, lambda k: q2(x, k, peer(dp, k, n_dp)).wait_recv())
-    pack = max(1, SUBLANES // rows)
-
-    def assemble(t):
-        for o in range(n_head):
-            piece = jnp.concatenate([qall[t * pack + u, o].astype(f32) for u in range(pack)], axis=0)
-            qf[pl.ds(t * pack * rows, pack * rows), o * width:(o + 1) * width] = piece
-
-    each(0, n_dp // pack, assemble)
-    qmat = qf[...].astype(bf16)
     sims = sim_scale * mm(u_both, qmat, NT)
     logits = sims[:docs]
     full = logits + sims[docs:]
-    pos_load.wait()
-    chosen = (pos_ref[...] == dp * docs + drow).astype(f32)
     top = jnp.max(logits, axis=0, keepdims=True)
     total = jnp.sum(jnp.exp(logits - top), axis=0, keepdims=True)
     hit = jnp.sum(logits * chosen, axis=0, keepdims=True)
@@ -234,21 +255,15 @@
     stat[dp] = jnp.where(srow == 0, top, jnp.where(srow == 1, total, hit))
     each(1, n_dp, lambda k: s_copy(k, dp).start())
 
-    qw_own[...] = mm(qmat, w_v[...], NT).astype(bf16)
-    qw_copy = remote(qw_own, qw_in, p_send.at[1], p_recv.at[1], "head", partner)
-    qw_copy.start()
-    uw = mm(u_both, w_v[...], NT)
-    uw = uw[:docs] + uw[docs:]
-    uw_own[...] = uw
+    uw = mm(u_both, w_half(1 - side), NT)
+    uw_own[...] = uw[:docs] + uw[docs:]
     uw_copy = remote(uw_own, uw_in, p_send.at[2], p_recv.at[2], "head", partner)
     uw_copy.start()
-
-    qw_copy.wait_recv()
-    qw = jnp.concatenate([qw_own[...], qw_in[...]], axis=1)
-    qw2 = jnp.concatenate([qw, qw], axis=0)
+    uw = mm(u_both, w_half(side), NT)
+    uw = uw[:docs] + uw[docs:]
     factor = rnorm * (loss_scale / len_f)
 
-    each(1, n_dp, lambda k: s_copy(k, peer(dp, k, n_dp)).wait_recv())
+    wait_all(stat.at[pl.ds(0, n_dp - 1)], s_recv)
     top = fold(
         n_dp, lambda k, c: jnp.maximum(c, stat[k][0:1]), jnp.full((1, nq), -jnp.inf, f32)
     )
@@ -269,21 +284,29 @@
     uw2 = jnp.concatenate([uw, uw_in[...]], axis=1)
     g = factor * (g - inner * uw2)
     small = jnp.concatenate(
-        [g[:, h * HD:(h + 1) * HD] for h in range(2 * heads)], axis=0
-    )
-    small = jnp.concatenate([small, small], axis=0).T
-    half = HD // 2
-    small = jnp.where(lax.rem(head, 2) == 0, small[:half], small[half:]).astype(bf16)
+        [g[:, h * half:(h + 1) * half] for h in range(2 * heads)], axis=0
+    )
+    small = jnp.concatenate([small, small], axis=0).T.astype(bf16)
     out_ref[...] = mm(small, a_ref[...], NN).astype(bf16)
 
-    each(1, n_head, lambda k: q1(k, head).wait_send())
-    for x in range(n_head):
-        each(1, n_dp, lambda k: q2(x, k, dp).wait_send())
-    each(1, n_head, lambda k: e_copy(k, head).wait_send())
-    each(1, n_dp, lambda k: s_copy(k, dp).wait_send())
+    wait_all(qall.at[0, pl.ds(0, n_head - 1)], q1_send)
+    wait_all(qall.at[pl.ds(0, n_dp - 1)], q2_send)
+    wait_all(emb_slot.at[pl.ds(0, n_head - 1)], e_send)
+    wait_all(stat.at[pl.ds(0, n_dp - 1)], s_send)
     c_copy.wait_send()
     qw_copy.wait_send()
     uw_copy.wait_send()
+
+
+def store(x_ref, l_ref, o_ref, lo_ref, sem):
+    copies = [
+        pltpu.make_async_copy(x_ref, o_ref, sem.at[0]),
+        pltpu.make_async_copy(l_ref, lo_ref, sem.at[1]),
+    ]
+    for copy in copies:
+        copy.start()
+    for copy in copies:
+        copy.wait()
 
 
 def per_device(n_dp, n_head, attn_queries, keys, values, out_weight, lengths, queries, positives):
@@ -294,6 +317,7 @@
     nq = n_dp * rows
     model = out_weight.shape[1]
     blocks = seq // LANES
+    half = width // 2
     dma = pltpu.SemaphoreType.DMA
     hbm = pl.BlockSpec(memory_space=pltpu.HBM)
     vmem = pl.BlockSpec(memory_space=pltpu.VMEM)
@@ -301,8 +325,8 @@
     d_values, loss = pl.pallas_call(
         functools.partial(kernel, n_dp, n_head),
         out_shape=(
-            jax.ShapeDtypeStruct((HD // 2, seq), bf16),
-            jax.ShapeDtypeStruct((1, 1), f32),
+            pltpu.VMEM((HD // 2, seq), bf16),
+            pltpu.SMEM((1, 1), f32),
         ),
         in_specs=[hbm, hbm, hbm, hbm, hbm, hbm, hbm],
         out_specs=(vmem, smem),
@@ -315,30 +339,42 @@
             pltpu.VMEM((width, model), bf16),
             pltpu.VMEM((n_dp, n_head, rows, width), bf16),
             pltpu.VMEM((nq, model), f32),
-            pltpu.VMEM((docs, seq), f32),
-            pltpu.VMEM((docs, seq), f32),
+            pltpu.VMEM((SUBLANES // 2, seq), f32),
+            pltpu.VMEM((SUBLANES // 2, seq), f32),
             pltpu.VMEM((n_head, docs, model), bf16),
             pltpu.VMEM((n_dp, SUBLANES // 2, nq), f32),
-            pltpu.VMEM((nq, width), bf16),
-            pltpu.VMEM((nq, width), bf16),
-            pltpu.VMEM((docs, width), f32),
-            pltpu.VMEM((docs, width), f32),
+            pltpu.VMEM((nq, half), bf16),
+            pltpu.VMEM((nq, half), bf16),
+            pltpu.VMEM((docs, half), f32),
+            pltpu.VMEM((docs, half), f32),
             pltpu.VMEM((4 * heads * docs, seq), bf16),
             dma((6,)),
             dma((blocks,)),
+            dma,
             dma((n_head,)),
+            dma,
             dma((n_head,)),
-            dma((n_head, n_dp)),
-            dma((n_head, n_dp)),
-            dma((n_head,)),
-            dma((n_head,)),
-            dma((n_dp,)),
-            dma((n_dp,)),
+            dma,
+            dma,
+            dma,
+            dma,
             dma((3,)),
             dma((3,)),
         ],
         compiler_params=pltpu.CompilerParams(collective_id=0, has_side_effects=True),
     )(lengths, positives.reshape(1, nq), attn_queries, keys, values, out_weight, queries)
+    d_values = pltpu.with_memory_space_constraint(d_values, pltpu.VMEM)
+    loss = pltpu.with_memory_space_constraint(loss, pltpu.SMEM)
+    d_values, loss = pl.pallas_call(
+        store,
+        out_shape=(
+            jax.ShapeDtypeStruct((HD // 2, seq), bf16),
+            jax.ShapeDtypeStruct((1, 1), f32),
+        ),
+        in_specs=[vmem, smem],
+        out_specs=(hbm, hbm),
+        scratch_shapes=[dma((2,))],
+    )(d_values, loss)
     return d_values.T, loss.reshape(())
 
 

time: 24.6 us -> 21.6 us (0.88)
  between operations: 2.39 us -> 0.64 us
  local copies, waits for them, and re-layouts: 1.47 us -> 0 us
  Pallas kernels: 20.5 us -> 20.8 us
    unnamed x1 -> x0, local copies, waits for them, and re-layouts: 1.47 us -> none
    pallas_call x1 -> x2, Pallas kernels: 20.5 us -> 20.8 us  [the longest x1 20.1 us: per_device(): pl.pallas_call(functools.partial(kernel, n_dp, n_head), out_shape=(pltpu....]
where the time goes in v1:
time: 21.6 us; the launch traced here: 21.4 us
  Pallas kernels  20.8 us (96%)
  between operations  0.64 us (3%)
    pallas_call x1, Pallas kernels, per_device(): pl.pallas_call(functools.partial(kernel, n_dp, n_head), out_shape=(pltpu....  20.1 us
    pallas_call x1, Pallas kernels, per_device(): pl.pallas_call(store, out_shape=(jax.ShapeDtypeStruct((HD // 2, seq), bf1...  0.66 us

profile of v1, /device:TPU:0, one launch (start us, length us, event | category | flops | bytes accessed | tf_op | source)
XLA Modules:
  0.0 21.4 jit_solution(527282738018121670)
XLA Ops:
  0.6 20.1 %shard_map.86 = (bf16[64,512]{1,0:T(8,128)(2,1)S(1)}, f32[1,1]{1,0:T(1,128)S(4)}) custom-call(s32[1,8]{1,0:T(1,128)} %lens_hbm.1, s32[1,32]{1,0:T(1,128)} %bitcast.3, bf16[512,384]{1,0:T(8,128)(2,1)} %q_hbm.1, bf16[512,256]{1,0:T(8,128)(2,1)} %k_hbm.1, bf16[512,256]{1,0:T(8,128)(2,1)} %v_hbm.1, bf16[384,1536]{1,0:T(8,128)(2,1)} %w_hbm.1, bf16[4,384]{1,0:T(4,128)(2,1)} %qry_hbm.1), custom_call_target="tpu_custom_call" | custom-call | tf_op jit(solution)/shard_map/pallas_call | solution.py:325
  20.8 0.7 %shard_map.87 = (bf16[64,512]{1,0:T(8,128)(2,1)}, f32[1,1]{1,0:T(1,128)}) custom-call(bf16[64,512]{1,0:T(8,128)(2,1)S(1)} %get-tuple-element.6.x_ref, f32[1,1]{1,0:T(1,128)S(4)} %get-tuple-element.7.l_ref), custom_call_target="tpu_custom_call" | custom-call | tf_op jit(solution)/shard_map/pallas_call | solution.py:368

commit v2 on v1

--- a/solution.py
+++ b/solution.py
@@ -13,6 +13,7 @@
 HD = 128
 LANES = 128
 SUBLANES = 8
+LONGEST = 256
 
 sim_scale = 20.0
 loss_scale = 32768.0
@@ -64,7 +65,7 @@
     lens_hbm, pos_hbm, q_hbm, k_hbm, v_hbm, w_hbm, qry_hbm,
     out_ref, loss_ref,
     lens, pos_ref, q_v, k_v, v_v, w_v, qall, qf, c_own, c_in, emb_slot, stat, qw_own, qw_in, uw_own, uw_in,
-    a_ref, load_sem, qload_sem, q1_send, q1_recv, q2_send, q2_recv, e_send, e_recv, s_send, s_recv,
+    a_ref, load_sem, qload_sem, q_send, q_recv, e_send, e_recv, s_send, s_recv,
     p_send, p_recv,
 ):
     dp = lax.axis_index("dp")
@@ -76,7 +77,7 @@
     half = HD // 2
     group = HEADS // KV_HEADS
     docs = lens.shape[1]
-    rows = qall.shape[2]
+    rows = qall.shape[1]
     nq = n_dp * rows
     kv_cols = pl.ds(pl.multiple_of((head * heads // group) * HD, HD), HD)
     blocks = seq // LANES
@@ -84,7 +85,7 @@
     k_load = pltpu.make_async_copy(k_hbm.at[:, kv_cols], k_v, load_sem.at[0])
     v_load = pltpu.make_async_copy(v_hbm.at[:, kv_cols], v_v, load_sem.at[1])
     w_load = pltpu.make_async_copy(w_hbm, w_v, load_sem.at[2])
-    qry_load = pltpu.make_async_copy(qry_hbm, qall.at[dp, head], load_sem.at[3])
+    qry_load = pltpu.make_async_copy(qry_hbm, qall.at[dp * n_head + head], load_sem.at[3])
     q_loads = [
         pltpu.make_async_copy(
             q_hbm.at[pl.ds(b * LANES, LANES)], q_v.at[pl.ds(b * LANES, LANES)], qload_sem.at[b]
@@ -108,27 +109,32 @@
     def peer(me, k, n):
         return lax.bitwise_xor(me, n - k)
 
-    def greet(axis, me, n):
-        def one(k):
-            pl.semaphore_signal(
-                barrier, inc=1, device_id={axis: peer(me, k, n)}, device_id_type=pl.DeviceIdType.MESH
-            )
-        each(1, n, one)
-
-    greet("head", head, n_head)
-    greet("dp", dp, n_dp)
-
-    def q1(k, owner):
-        slot = qall.at[dp, owner]
-        return remote(slot, slot, q1_send, q1_recv.at[k], "head", peer(head, k, n_head))
-
-    def q2(x, k, owner):
-        slot = qall.at[owner, lax.bitwise_xor(head, x)]
-        return remote(slot, slot, q2_send, q2_recv.at[x], "dp", peer(dp, k, n_dp))
-
-    def e_copy(k, owner):
-        slot = emb_slot.at[owner]
-        return remote(slot, slot, e_send, e_recv, "head", peer(head, k, n_head))
+    def everyone(body):
+        for x in reversed(range(n_head)):
+            each(0 if x else 1, n_dp, lambda k: body(lax.bitwise_xor(head, x), lax.bitwise_xor(dp, n_dp - 1 - k) if x else lax.bitwise_xor(dp, n_dp - k)))
+
+    everyone(lambda h, d: pl.semaphore_signal(
+        barrier, inc=1, device_id={"dp": d, "head": h}, device_id_type=pl.DeviceIdType.MESH
+    ))
+    peers = n_dp * n_head - 1
+    mine = qall.at[dp * n_head + head]
+
+    def q_copy(h, d):
+        return pltpu.make_async_remote_copy(
+            src_ref=mine, dst_ref=mine, send_sem=q_send, recv_sem=q_recv,
+            device_id={"dp": d, "head": h}, device_id_type=pl.DeviceIdType.MESH,
+        )
+
+    def queries_to(h):
+        @pl.when(head != h)
+        def _():
+            q_copy(h, dp).start()
+
+        each(1, n_dp, lambda k: q_copy(h, peer(dp, k, n_dp)).start())
+
+    def e_copy(h):
+        slot = emb_slot.at[head]
+        return remote(slot, slot, e_send, e_recv, "head", h)
 
     def s_copy(k, owner):
         slot = stat.at[owner]
@@ -150,34 +156,39 @@
     member = (ii >= starts) & (ii < starts + lens_col)
 
     k_load.wait()
-    ones = jnp.ones((docs, LANES), bf16)
     rate = math.log2(math.e) / math.sqrt(HD)
-    sums = [[None] * blocks for _ in range(heads)]
+    reach = (LONGEST + LANES - 2) // LANES
+    weights = [[None] * blocks for _ in range(heads)]
     for b in range(blocks):
         q_loads[b].wait()
-        n = (b + 1) * LANES
-        cols = slice(b * LANES, n)
-        jj = lax.broadcasted_iota(jnp.int32, (n, LANES), 0)
-        allowed = (jj >= start_row[:, cols]) & (jj <= ii[:, cols])
-        keys = k_v[:n, :]
+        cols = slice(b * LANES, (b + 1) * LANES)
+        first = max(0, b - reach)
+        allowed = []
+        for j in range(first, b + 1):
+            jj = lax.broadcasted_iota(jnp.int32, (LANES, LANES), 0) + j * LANES
+            ok = jj >= start_row[:, cols]
+            allowed.append(ok & (jj <= ii[:, cols]) if j == b else ok)
+        allowed = jnp.concatenate(allowed, axis=0)
         for h in range(heads):
-            s = mm(keys, q_v[cols, h * HD:(h + 1) * HD], NT)
+            s = mm(k_v[first * LANES:(b + 1) * LANES, :], q_v[cols, h * HD:(h + 1) * HD], NT)
             s = jnp.where(allowed, s, -1e30)
             e = jnp.exp2((s - jnp.max(s, axis=0, keepdims=True)) * rate)
-            p = (e * (1.0 / jnp.sum(e, axis=0, keepdims=True))).astype(bf16)
-            part = mm(ones, p, NT)
-            for j in range(b + 1):
-                piece = part[:, j * LANES:(j + 1) * LANES]
-                sums[h][j] = piece if sums[h][j] is None else sums[h][j] + piece
-        if b == 1:
-            qry_load.wait()
-            pl.semaphore_wait(barrier, n_head - 1 + n_dp - 1)
-            each(1, n_head, lambda k: q1(k, head).start())
-            each(1, n_dp, lambda k: q2(0, k, dp).start())
-
-    csum = [jnp.concatenate(sums[h], axis=1) for h in range(heads)]
+            p = e * (1.0 / jnp.sum(e, axis=0, keepdims=True))
+            for j in range(first, b + 1):
+                piece = p[(j - first) * LANES:(j - first + 1) * LANES]
+                weights[h][j] = piece if weights[h][j] is None else weights[h][j] + piece
+
+    def keys_of(x):
+        x = jnp.sum(x.T, axis=0, keepdims=True)
+        return jnp.broadcast_to(x, (docs, LANES))
+
+    csum = [jnp.concatenate([keys_of(x) for x in weights[h]], axis=1) for h in range(heads)]
     spread = jnp.concatenate([jnp.where(member, csum[h], 0.0) for h in range(heads)], axis=0)
     s_hi, s_lo = hi_lo(spread)
+    qry_load.wait()
+    pl.semaphore_wait(barrier, peers)
+    queries_to(0)
+    queries_to(1)
     v_load.wait()
     span = heads * docs
     pooled = mm(jnp.concatenate([s_hi, s_lo], axis=0), v_v[...], NN)
@@ -189,7 +200,13 @@
     w_load.wait()
     emb = mm(jnp.concatenate([p_hi, p_lo], axis=0), w_v[...], NN)
     emb_slot[head] = (emb[:docs] + emb[docs:]).astype(bf16)
-    each(1, n_head, lambda k: e_copy(k, head).start())
+    for h in range(n_head):
+        @pl.when(head != h)
+        def _():
+            e_copy(h).start()
+
+    for h in range(2, n_head):
+        queries_to(h)
 
     rid = lax.broadcasted_iota(jnp.int32, (c_own.shape[0], 1), 0)
     packed = jnp.zeros(c_own.shape, f32)
@@ -198,17 +215,12 @@
     c_own[...] = packed
     c_copy = remote(c_own, c_in, p_send.at[0], p_recv.at[0], "head", partner)
     c_copy.start()
-    for x in range(1, n_head):
-        q1(n_head - x, lax.bitwise_xor(head, x)).wait_recv()
-        each(1, n_dp, lambda k: q2(x, k, dp).start())
-
-    for x in range(n_head):
-        wait_all(qall.at[pl.ds(0, n_dp - 1), 0], q2_recv.at[x])
+    wait_all(qall.at[pl.ds(0, peers)], q_recv)
     pack = max(1, SUBLANES // rows)
 
     def assemble(t):
         for o in range(n_head):
-            piece = jnp.concatenate([qall[t * pack + u, o].astype(f32) for u in range(pack)], axis=0)
+            piece = jnp.concatenate([qall[(t * pack + u) * n_head + o].astype(f32) for u in range(pack)], axis=0)
             qf[pl.ds(t * pack * rows, pack * rows), o * width:(o + 1) * width] = piece
 
     each(0, n_dp // pack, assemble)
@@ -219,21 +231,6 @@
             [w_v[pl.ds(pl.multiple_of(h * HD + which * half, half), half), :] for h in range(heads)], axis=0
         )
 
-    qw_own[...] = mm(qmat, w_half(1 - side), NT).astype(bf16)
-    qw_copy = remote(qw_own, qw_in, p_send.at[1], p_recv.at[1], "head", partner)
-    qw_copy.start()
-    qw_mine = mm(qmat, w_half(side), NT).astype(bf16)
-
-    c_copy.wait_recv()
-    other = jnp.concatenate(
-        [jnp.where(member, c_in[h:h + 1, :], 0.0) for h in range(heads)], axis=0
-    )
-    both = jnp.concatenate([spread, other], axis=0)
-    b_hi, b_lo = hi_lo(both)
-    a_ref[...] = jnp.concatenate([b_hi, b_lo], axis=0)
-    qw_copy.wait_recv()
-    qw = jnp.concatenate([qw_mine, qw_in[...]], axis=1)
-    qw2 = jnp.concatenate([qw, qw], axis=0)
     pos_load.wait()
     chosen = (pos_ref[...] == dp * docs + drow).astype(f32)
 
@@ -255,13 +252,26 @@
     stat[dp] = jnp.where(srow == 0, top, jnp.where(srow == 1, total, hit))
     each(1, n_dp, lambda k: s_copy(k, dp).start())
 
-    uw = mm(u_both, w_half(1 - side), NT)
-    uw_own[...] = uw[:docs] + uw[docs:]
+    lhs = jnp.concatenate([qmat, u_both], axis=0)
+    proj = mm(lhs, w_half(1 - side), NT)
+    qw_own[...] = proj[:nq].astype(bf16)
+    qw_copy = remote(qw_own, qw_in, p_send.at[1], p_recv.at[1], "head", partner)
+    qw_copy.start()
+    uw_own[...] = proj[nq:nq + docs] + proj[nq + docs:]
     uw_copy = remote(uw_own, uw_in, p_send.at[2], p_recv.at[2], "head", partner)
     uw_copy.start()
-    uw = mm(u_both, w_half(side), NT)
-    uw = uw[:docs] + uw[docs:]
+    proj = mm(lhs, w_half(side), NT)
+    qw_mine = proj[:nq].astype(bf16)
+    uw = proj[nq:nq + docs] + proj[nq + docs:]
     factor = rnorm * (loss_scale / len_f)
+
+    c_copy.wait_recv()
+    other = jnp.concatenate(
+        [jnp.where(member, c_in[h:h + 1, :], 0.0) for h in range(heads)], axis=0
+    )
+    both = jnp.concatenate([spread, other], axis=0)
+    b_hi, b_lo = hi_lo(both)
+    a_ref[...] = jnp.concatenate([b_hi, b_lo], axis=0)
 
     wait_all(stat.at[pl.ds(0, n_dp - 1)], s_recv)
     top = fold(
@@ -279,6 +289,9 @@
     dl = jnp.exp(logits - lse) - chosen
     inner = jnp.sum(dl * full, axis=1, keepdims=True)
     d_hi, d_lo = hi_lo(dl)
+    qw_copy.wait_recv()
+    qw = jnp.concatenate([qw_mine, qw_in[...]], axis=1)
+    qw2 = jnp.concatenate([qw, qw], axis=0)
     g = sim_scale * mm(jnp.concatenate([d_hi, d_lo], axis=1), qw2, NN)
     uw_copy.wait_recv()
     uw2 = jnp.concatenate([uw, uw_in[...]], axis=1)
@@ -289,8 +302,7 @@
     small = jnp.concatenate([small, small], axis=0).T.astype(bf16)
     out_ref[...] = mm(small, a_ref[...], NN).astype(bf16)
 
-    wait_all(qall.at[0, pl.ds(0, n_head - 1)], q1_send)
-    wait_all(qall.at[pl.ds(0, n_dp - 1)], q2_send)
+    wait_all(qall.at[pl.ds(0, peers)], q_send)
     wait_all(emb_slot.at[pl.ds(0, n_head - 1)], e_send)
     wait_all(stat.at[pl.ds(0, n_dp - 1)], s_send)
     c_copy.wait_send()
@@ -337,7 +349,7 @@
             pltpu.VMEM((seq, HD), bf16),
             pltpu.VMEM((seq, HD), bf16),
             pltpu.VMEM((width, model), bf16),
-            pltpu.VMEM((n_dp, n_head, rows, width), bf16),
+            pltpu.VMEM((n_dp * n_head, rows, width), bf16),
             pltpu.VMEM((nq, model), f32),
             pltpu.VMEM((SUBLANES // 2, seq), f32),
             pltpu.VMEM((SUBLANES // 2, seq), f32),
@@ -351,9 +363,7 @@
             dma((6,)),
             dma((blocks,)),
             dma,
-            dma((n_head,)),
-            dma,
-            dma((n_head,)),
+            dma,
             dma,
             dma,
             dma,

time: 21.6 us -> 18.1 us (0.84)
  Pallas kernels: 20.8 us -> 17.3 us
    pallas_call x1, Pallas kernels: 20.1 us -> 16.6 us  [per_device(): pl.pallas_call(functools.partial(kernel, n_dp, n_head), out_shape=(pltpu....]
where the time goes in v2:
time: 18.1 us; the launch traced here: 17.9 us
  Pallas kernels  17.3 us (96%)
  between operations  0.64 us (4%)
    pallas_call x1, Pallas kernels, per_device(): pl.pallas_call(functools.partial(kernel, n_dp, n_head), out_shape=(pltpu....  16.6 us
    pallas_call x1, Pallas kernels, per_device(): pl.pallas_call(store, out_shape=(jax.ShapeDtypeStruct((HD // 2, seq), bf1...  0.66 us

profile of v2, /device:TPU:0, one launch (start us, length us, event | category | flops | bytes accessed | tf_op | source)
XLA Modules:
  0.0 17.9 jit_solution(11498335777130830530)
XLA Ops:
  0.6 16.6 %shard_map.86 = (bf16[64,512]{1,0:T(8,128)(2,1)S(1)}, f32[1,1]{1,0:T(1,128)S(4)}) custom-call(s32[1,8]{1,0:T(1,128)} %lens_hbm.1, s32[1,32]{1,0:T(1,128)} %bitcast.3, bf16[512,384]{1,0:T(8,128)(2,1)} %q_hbm.1, bf16[512,256]{1,0:T(8,128)(2,1)} %k_hbm.1, bf16[512,256]{1,0:T(8,128)(2,1)} %v_hbm.1, bf16[384,1536]{1,0:T(8,128)(2,1)} %w_hbm.1, bf16[4,384]{1,0:T(4,128)(2,1)} %qry_hbm.1), custom_call_target="tpu_custom_call" | custom-call | tf_op jit(solution)/shard_map/pallas_call | solution.py:337
  17.3 0.7 %shard_map.87 = (bf16[64,512]{1,0:T(8,128)(2,1)}, f32[1,1]{1,0:T(1,128)}) custom-call(bf16[64,512]{1,0:T(8,128)(2,1)S(1)} %get-tuple-element.6.x_ref, f32[1,1]{1,0:T(1,128)S(4)} %get-tuple-element.7.l_ref), custom_call_target="tpu_custom_call" | custom-call | tf_op jit(solution)/shard_map/pallas_call | solution.py:378

commit v3 on v2

--- a/solution.py
+++ b/solution.py
@@ -65,7 +65,7 @@
     lens_hbm, pos_hbm, q_hbm, k_hbm, v_hbm, w_hbm, qry_hbm,
     out_ref, loss_ref,
     lens, pos_ref, q_v, k_v, v_v, w_v, qall, qf, c_own, c_in, emb_slot, stat, qw_own, qw_in, uw_own, uw_in,
-    a_ref, load_sem, qload_sem, q_send, q_recv, e_send, e_recv, s_send, s_recv,
+    a_ref, e_sum, hello, load_sem, qload_sem, q_send, q_recv, e_send, e_recv, s_send, s_recv,
     p_send, p_recv,
 ):
     dp = lax.axis_index("dp")
@@ -86,20 +86,13 @@
     v_load = pltpu.make_async_copy(v_hbm.at[:, kv_cols], v_v, load_sem.at[1])
     w_load = pltpu.make_async_copy(w_hbm, w_v, load_sem.at[2])
     qry_load = pltpu.make_async_copy(qry_hbm, qall.at[dp * n_head + head], load_sem.at[3])
-    q_loads = [
-        pltpu.make_async_copy(
-            q_hbm.at[pl.ds(b * LANES, LANES)], q_v.at[pl.ds(b * LANES, LANES)], qload_sem.at[b]
-        )
-        for b in range(blocks)
-    ]
+    q_load = pltpu.make_async_copy(q_hbm, q_v, qload_sem)
     lens_load = pltpu.make_async_copy(lens_hbm, lens, load_sem.at[4])
     pos_load = pltpu.make_async_copy(pos_hbm, pos_ref, load_sem.at[5])
     lens_load.start()
     k_load.start()
-    q_loads[0].start()
     qry_load.start()
-    for load in q_loads[1:]:
-        load.start()
+    q_load.start()
     v_load.start()
     w_load.start()
     pos_load.start()
@@ -109,13 +102,17 @@
     def peer(me, k, n):
         return lax.bitwise_xor(me, n - k)
 
-    def everyone(body):
-        for x in reversed(range(n_head)):
-            each(0 if x else 1, n_dp, lambda k: body(lax.bitwise_xor(head, x), lax.bitwise_xor(dp, n_dp - 1 - k) if x else lax.bitwise_xor(dp, n_dp - k)))
-
-    everyone(lambda h, d: pl.semaphore_signal(
-        barrier, inc=1, device_id={"dp": d, "head": h}, device_id_type=pl.DeviceIdType.MESH
-    ))
+    rank = head * n_dp + dp
+
+    def ranks(first, last, body):
+        lax.fori_loop(first, last, lambda f, c: (body(lax.div(f, n_dp), lax.rem(f, n_dp)), c)[1], 0)
+
+    def signal(semaphore, h, d):
+        pl.semaphore_signal(
+            semaphore, inc=1, device_id={"dp": d, "head": h}, device_id_type=pl.DeviceIdType.MESH
+        )
+
+    ranks(rank + 1, n_dp * n_head, lambda h, d: signal(barrier, h, d))
     peers = n_dp * n_head - 1
     mine = qall.at[dp * n_head + head]
 
@@ -125,20 +122,37 @@
             device_id={"dp": d, "head": h}, device_id_type=pl.DeviceIdType.MESH,
         )
 
-    def queries_to(h):
-        @pl.when(head != h)
-        def _():
-            q_copy(h, dp).start()
-
-        each(1, n_dp, lambda k: q_copy(h, peer(dp, k, n_dp)).start())
-
     def e_copy(h):
         slot = emb_slot.at[head]
-        return remote(slot, slot, e_send, e_recv, "head", h)
+        return remote(slot, slot, e_send, e_recv.at[head], "head", h)
+
+    def e_from(h):
+        return remote(emb_slot.at[h], emb_slot.at[h], e_send, e_recv.at[h], "head", h)
+
+    def sum_copy(h):
+        return remote(e_sum, emb_slot.at[1], e_send, e_recv.at[1], "head", h)
 
     def s_copy(k, owner):
         slot = stat.at[owner]
         return remote(slot, slot, s_send, s_recv, "dp", peer(dp, k, n_dp))
+
+    def queries(first, last):
+        ranks(first, last, lambda h, d: q_copy(h, d).start())
+
+    far = dp >= n_dp // 4
+
+    def meet():
+        @pl.when(rank > 0)
+        def _():
+            pl.semaphore_wait(barrier, rank)
+
+        ranks(0, rank, lambda h, d: signal(hello.at[head], h, d))
+        qry_load.wait()
+
+    @pl.when(far)
+    def _():
+        meet()
+        ranks(0, jnp.minimum(rank, 2 * n_dp), lambda h, d: q_copy(h, d).start())
 
     ii = lax.broadcasted_iota(jnp.int32, (1, seq), 1)
     drow = lax.broadcasted_iota(jnp.int32, (docs, 1), 0)
@@ -159,8 +173,8 @@
     rate = math.log2(math.e) / math.sqrt(HD)
     reach = (LONGEST + LANES - 2) // LANES
     weights = [[None] * blocks for _ in range(heads)]
+    q_load.wait()
     for b in range(blocks):
-        q_loads[b].wait()
         cols = slice(b * LANES, (b + 1) * LANES)
         first = max(0, b - reach)
         allowed = []
@@ -185,10 +199,6 @@
     csum = [jnp.concatenate([keys_of(x) for x in weights[h]], axis=1) for h in range(heads)]
     spread = jnp.concatenate([jnp.where(member, csum[h], 0.0) for h in range(heads)], axis=0)
     s_hi, s_lo = hi_lo(spread)
-    qry_load.wait()
-    pl.semaphore_wait(barrier, peers)
-    queries_to(0)
-    queries_to(1)
     v_load.wait()
     span = heads * docs
     pooled = mm(jnp.concatenate([s_hi, s_lo], axis=0), v_v[...], NN)
@@ -200,13 +210,50 @@
     w_load.wait()
     emb = mm(jnp.concatenate([p_hi, p_lo], axis=0), w_v[...], NN)
     emb_slot[head] = (emb[:docs] + emb[docs:]).astype(bf16)
-    for h in range(n_head):
-        @pl.when(head != h)
+    pl.when(jnp.logical_not(far))(meet)
+    ahead = jnp.logical_and(head >= 2, jnp.logical_not(far))
+
+    @pl.when(ahead)
+    def _():
+        queries(0, n_dp)
+        e_copy(1).start()
+        queries(n_dp, 2 * n_dp)
+        e_copy(0).start()
+
+    def plane(t, carry):
+        base = t * n_dp
+        inside = t == head
+
+        @pl.when(t > head)
         def _():
-            e_copy(h).start()
-
-    for h in range(2, n_head):
-        queries_to(h)
+            pl.semaphore_wait(hello.at[t], n_dp)
+
+        @pl.when(jnp.logical_and(t != head, jnp.logical_or(t < head, jnp.logical_or(head >= 2, t + head == 1))))
+        def _():
+            e_copy(t).start()
+
+        last = jnp.where(inside, dp, n_dp)
+        sent = jnp.logical_and(far, jnp.logical_and(t < 2, t <= head))
+        ranks(base, base + jnp.where(sent, 0, last), lambda h, d: q_copy(h, d).start())
+
+        @pl.when(jnp.logical_and(inside, dp < n_dp - 1))
+        def _():
+            pl.semaphore_wait(hello.at[t], n_dp - 1 - dp)
+            ranks(base + dp + 1, base + n_dp, lambda h, d: q_copy(h, d).start())
+
+        return carry
+
+    lax.fori_loop(jnp.where(ahead, 2, 0), n_head, plane, 0)
+
+    @pl.when(head == 1)
+    def _():
+        e_from(0).wait_recv()
+        e_sum[...] = (emb_slot[0].astype(f32) + emb_slot[1].astype(f32)).astype(bf16)
+        each(2, n_head, lambda h: sum_copy(h).start())
+
+    @pl.when(head >= 2)
+    def _():
+        emb_slot[0] = jnp.zeros(emb_slot.shape[1:], bf16)
 
     rid = lax.broadcasted_iota(jnp.int32, (c_own.shape[0], 1), 0)
     packed = jnp.zeros(c_own.shape, f32)
@@ -234,7 +281,10 @@
     pos_load.wait()
     chosen = (pos_ref[...] == dp * docs + drow).astype(f32)
 
-    wait_all(emb_slot.at[pl.ds(0, n_head - 1)], e_recv)
+    pl.when(head == 0)(lambda: e_from(1).wait_recv())
+    pl.when(head >= 2)(lambda: e_from(1).wait_recv())
+    for h in range(2, n_head):
+        pl.when(head != h)(lambda: e_from(h).wait_recv())
     emb = emb_slot[0].astype(f32)
     for o in range(1, n_head):
         emb = emb + emb_slot[o].astype(f32)
@@ -242,6 +292,18 @@
     unit = emb * rnorm
     u_hi, u_lo = hi_lo(unit)
     u_both = jnp.concatenate([u_hi, u_lo], axis=0)
+    lhs = jnp.concatenate([qmat, u_both], axis=0)
+    qw_copy = remote(qw_own, qw_in, p_send.at[1], p_recv.at[1], "head", partner)
+    uw_copy = remote(uw_own, uw_in, p_send.at[2], p_recv.at[2], "head", partner)
+
+    def project():
+        proj = mm(lhs, w_half(1 - side), NT)
+        qw_own[...] = proj[:nq].astype(bf16)
+        qw_copy.start()
+        uw_own[...] = proj[nq:nq + docs] + proj[nq + docs:]
+        uw_copy.start()
+
+    pl.when(side == 1)(project)
     sims = sim_scale * mm(u_both, qmat, NT)
     logits = sims[:docs]
     full = logits + sims[docs:]
@@ -252,14 +314,7 @@
     stat[dp] = jnp.where(srow == 0, top, jnp.where(srow == 1, total, hit))
     each(1, n_dp, lambda k: s_copy(k, dp).start())
 
-    lhs = jnp.concatenate([qmat, u_both], axis=0)
-    proj = mm(lhs, w_half(1 - side), NT)
-    qw_own[...] = proj[:nq].astype(bf16)
-    qw_copy = remote(qw_own, qw_in, p_send.at[1], p_recv.at[1], "head", partner)
-    qw_copy.start()
-    uw_own[...] = proj[nq:nq + docs] + proj[nq + docs:]
-    uw_copy = remote(uw_own, uw_in, p_send.at[2], p_recv.at[2], "head", partner)
-    uw_copy.start()
+    pl.when(side == 0)(project)
     proj = mm(lhs, w_half(side), NT)
     qw_mine = proj[:nq].astype(bf16)
     uw = proj[nq:nq + docs] + proj[nq + docs:]
@@ -273,10 +328,18 @@
     b_hi, b_lo = hi_lo(both)
     a_ref[...] = jnp.concatenate([b_hi, b_lo], axis=0)
 
+    qw_copy.wait_recv()
+    qw = jnp.concatenate([qw_mine, qw_in[...]], axis=1)
+    qw2 = jnp.concatenate([qw, qw], axis=0)
+    uw_copy.wait_recv()
+    uw2 = factor * jnp.concatenate([uw, uw_in[...]], axis=1)
+    factor = factor * sim_scale
+
     wait_all(stat.at[pl.ds(0, n_dp - 1)], s_recv)
     top = fold(
         n_dp, lambda k, c: jnp.maximum(c, stat[k][0:1]), jnp.full((1, nq), -jnp.inf, f32)
     )
+    shifted = jnp.exp(logits - top)
 
     def gather(k, c):
         tile = stat[k]
@@ -284,18 +347,12 @@
 
     zero = jnp.zeros((1, nq), f32)
     total, hit = fold(n_dp, gather, (zero, zero))
-    lse = top + jnp.log(total)
-    loss_ref[0, 0] = jnp.sum(lse - hit) * (1.0 / nq)
-    dl = jnp.exp(logits - lse) - chosen
+    dl = shifted * (1.0 / total) - chosen
+    d_hi, d_lo = hi_lo(dl)
+    g = mm(jnp.concatenate([d_hi, d_lo], axis=1), qw2, NN)
     inner = jnp.sum(dl * full, axis=1, keepdims=True)
-    d_hi, d_lo = hi_lo(dl)
-    qw_copy.wait_recv()
-    qw = jnp.concatenate([qw_mine, qw_in[...]], axis=1)
-    qw2 = jnp.concatenate([qw, qw], axis=0)
-    g = sim_scale * mm(jnp.concatenate([d_hi, d_lo], axis=1), qw2, NN)
-    uw_copy.wait_recv()
-    uw2 = jnp.concatenate([uw, uw_in[...]], axis=1)
-    g = factor * (g - inner * uw2)
+    loss_ref[0, 0] = jnp.sum(top + jnp.log(total) - hit) * (1.0 / nq)
+    g = factor * g - inner * uw2
     small = jnp.concatenate(
         [g[:, h * half:(h + 1) * half] for h in range(2 * heads)], axis=0
     )
@@ -303,7 +360,8 @@
     out_ref[...] = mm(small, a_ref[...], NN).astype(bf16)
 
     wait_all(qall.at[pl.ds(0, peers)], q_send)
-    wait_all(emb_slot.at[pl.ds(0, n_head - 1)], e_send)
+    pl.when(head == 0)(lambda: wait_all(emb_slot.at[0], e_send))
+    pl.when(head > 0)(lambda: wait_all(emb_slot.at[pl.ds(0, n_head - 1)], e_send))
     wait_all(stat.at[pl.ds(0, n_dp - 1)], s_send)
     c_copy.wait_send()
     qw_copy.wait_send()
@@ -360,12 +418,14 @@
             pltpu.VMEM((docs, half), f32),
             pltpu.VMEM((docs, half), f32),
             pltpu.VMEM((4 * heads * docs, seq), bf16),
+            pltpu.VMEM((docs, model), bf16),
+            pltpu.SemaphoreType.REGULAR((n_head,)),
             dma((6,)),
-            dma((blocks,)),
-            dma,
-            dma,
-            dma,
-            dma,
+            dma,
+            dma,
+            dma,
+            dma,
+            dma((n_head,)),
             dma,
             dma,
             dma((3,)),

time: 18.1 us -> 16.4 us (0.906)
  Pallas kernels: 17.3 us -> 15.6 us
    pallas_call x1, Pallas kernels: 16.6 us -> 14.9 us  [per_device(): pl.pallas_call(functools.partial(kernel, n_dp, n_head), out_shape=(pltpu....]
where the time goes in v3:
time: 16.4 us; the launch traced here: 16.2 us
  Pallas kernels  15.6 us (95%)
  between operations  0.64 us (4%)
    pallas_call x1, Pallas kernels, per_device(): pl.pallas_call(functools.partial(kernel, n_dp, n_head), out_shape=(pltpu....  14.9 us
    pallas_call x1, Pallas kernels, per_device(): pl.pallas_call(store, out_shape=(jax.ShapeDtypeStruct((HD // 2, seq), bf1...  0.66 us

profile of v3, /device:TPU:0, one launch (start us, length us, event | category | flops | bytes accessed | tf_op | source)
XLA Modules:
  0.0 16.2 jit_solution(11687354818440593109)
XLA Ops:
  0.6 14.9 %shard_map.86 = (bf16[64,512]{1,0:T(8,128)(2,1)S(1)}, f32[1,1]{1,0:T(1,128)S(4)}) custom-call(s32[1,8]{1,0:T(1,128)} %lens_hbm.1, s32[1,32]{1,0:T(1,128)} %bitcast.3, bf16[512,384]{1,0:T(8,128)(2,1)} %q_hbm.1, bf16[512,256]{1,0:T(8,128)(2,1)} %k_hbm.1, bf16[512,256]{1,0:T(8,128)(2,1)} %v_hbm.1, bf16[384,1536]{1,0:T(8,128)(2,1)} %w_hbm.1, bf16[4,384]{1,0:T(4,128)(2,1)} %qry_hbm.1), custom_call_target="tpu_custom_call" | custom-call | tf_op jit(solution)/shard_map/pallas_call | solution.py:395
  15.6 0.7 %shard_map.87 = (bf16[64,512]{1,0:T(8,128)(2,1)}, f32[1,1]{1,0:T(1,128)}) custom-call(bf16[64,512]{1,0:T(8,128)(2,1)S(1)} %get-tuple-element.6.x_ref, f32[1,1]{1,0:T(1,128)S(4)} %get-tuple-element.7.l_ref), custom_call_target="tpu_custom_call" | custom-call | tf_op jit(solution)/shard_map/pallas_call | solution.py:438

commit v4 on v3

--- a/solution.py
+++ b/solution.py
@@ -65,8 +65,8 @@
     lens_hbm, pos_hbm, q_hbm, k_hbm, v_hbm, w_hbm, qry_hbm,
     out_ref, loss_ref,
     lens, pos_ref, q_v, k_v, v_v, w_v, qall, qf, c_own, c_in, emb_slot, stat, qw_own, qw_in, uw_own, uw_in,
-    a_ref, e_sum, hello, load_sem, qload_sem, q_send, q_recv, e_send, e_recv, s_send, s_recv,
-    p_send, p_recv,
+    a_ref, e_sum, hello, load_sem, qload_sem, send, q_recv, e_recv, s_recv,
+    p_recv,
 ):
     dp = lax.axis_index("dp")
     head = lax.axis_index("head")
@@ -88,7 +88,7 @@
     qry_load = pltpu.make_async_copy(qry_hbm, qall.at[dp * n_head + head], load_sem.at[3])
     q_load = pltpu.make_async_copy(q_hbm, q_v, qload_sem)
     lens_load = pltpu.make_async_copy(lens_hbm, lens, load_sem.at[4])
-    pos_load = pltpu.make_async_copy(pos_hbm, pos_ref, load_sem.at[5])
+    pos_load = pltpu.make_async_copy(pos_hbm, pos_ref, load_sem.at[1])
     lens_load.start()
     k_load.start()
     qry_load.start()
@@ -118,23 +118,23 @@
 
     def q_copy(h, d):
         return pltpu.make_async_remote_copy(
-            src_ref=mine, dst_ref=mine, send_sem=q_send, recv_sem=q_recv,
+            src_ref=mine, dst_ref=mine, send_sem=send, recv_sem=q_recv,
             device_id={"dp": d, "head": h}, device_id_type=pl.DeviceIdType.MESH,
         )
 
     def e_copy(h):
         slot = emb_slot.at[head]
-        return remote(slot, slot, e_send, e_recv.at[head], "head", h)
+        return remote(slot, slot, send, e_recv.at[jnp.minimum(head, 1)], "head", h)
 
     def e_from(h):
-        return remote(emb_slot.at[h], emb_slot.at[h], e_send, e_recv.at[h], "head", h)
+        return remote(emb_slot.at[h], emb_slot.at[h], send, e_recv.at[min(h, 1)], "head", h)
 
     def sum_copy(h):
-        return remote(e_sum, emb_slot.at[1], e_send, e_recv.at[1], "head", h)
+        return remote(e_sum, emb_slot.at[1], send, e_recv.at[1], "head", h)
 
     def s_copy(k, owner):
         slot = stat.at[owner]
-        return remote(slot, slot, s_send, s_recv, "dp", peer(dp, k, n_dp))
+        return remote(slot, slot, send, s_recv, "dp", peer(dp, k, n_dp))
 
     def queries(first, last):
         ranks(first, last, lambda h, d: q_copy(h, d).start())
@@ -146,12 +146,14 @@
         def _():
             pl.semaphore_wait(barrier, rank)
 
+    def greet():
         ranks(0, rank, lambda h, d: signal(hello.at[head], h, d))
-        qry_load.wait()
 
     @pl.when(far)
     def _():
         meet()
+        greet()
+        qry_load.wait()
         ranks(0, jnp.minimum(rank, 2 * n_dp), lambda h, d: q_copy(h, d).start())
 
     ii = lax.broadcasted_iota(jnp.int32, (1, seq), 1)
@@ -200,6 +202,7 @@
     spread = jnp.concatenate([jnp.where(member, csum[h], 0.0) for h in range(heads)], axis=0)
     s_hi, s_lo = hi_lo(spread)
     v_load.wait()
+    pos_load.wait()
     span = heads * docs
     pooled = mm(jnp.concatenate([s_hi, s_lo], axis=0), v_v[...], NN)
     pooled = pooled[:span] + pooled[span:]
@@ -210,15 +213,22 @@
     w_load.wait()
     emb = mm(jnp.concatenate([p_hi, p_lo], axis=0), w_v[...], NN)
     emb_slot[head] = (emb[:docs] + emb[docs:]).astype(bf16)
-    pl.when(jnp.logical_not(far))(meet)
+    @pl.when(jnp.logical_not(far))
+    def _():
+        meet()
+        qry_load.wait()
+
     ahead = jnp.logical_and(head >= 2, jnp.logical_not(far))
 
     @pl.when(ahead)
     def _():
         queries(0, n_dp)
         e_copy(1).start()
+        greet()
         queries(n_dp, 2 * n_dp)
         e_copy(0).start()
+
+    pl.when(jnp.logical_and(head < 2, jnp.logical_not(far)))(greet)
 
     def plane(t, carry):
         base = t * n_dp
@@ -260,7 +270,7 @@
     for h in range(heads):
         packed = jnp.where(rid == h, csum[h][:c_own.shape[0]], packed)
     c_own[...] = packed
-    c_copy = remote(c_own, c_in, p_send.at[0], p_recv.at[0], "head", partner)
+    c_copy = remote(c_own, c_in, send, p_recv.at[0], "head", partner)
     c_copy.start()
     wait_all(qall.at[pl.ds(0, peers)], q_recv)
     pack = max(1, SUBLANES // rows)
@@ -278,35 +288,29 @@
             [w_v[pl.ds(pl.multiple_of(h * HD + which * half, half), half), :] for h in range(heads)], axis=0
         )
 
-    pos_load.wait()
     chosen = (pos_ref[...] == dp * docs + drow).astype(f32)
 
-    pl.when(head == 0)(lambda: e_from(1).wait_recv())
-    pl.when(head >= 2)(lambda: e_from(1).wait_recv())
-    for h in range(2, n_head):
-        pl.when(head != h)(lambda: e_from(h).wait_recv())
+    pl.when(head == 0)(lambda: wait_all(emb_slot.at[pl.ds(0, n_head - 1)], e_recv.at[1]))
+    pl.when(head > 0)(lambda: wait_all(emb_slot.at[pl.ds(0, n_head - 2)], e_recv.at[1]))
     emb = emb_slot[0].astype(f32)
     for o in range(1, n_head):
         emb = emb + emb_slot[o].astype(f32)
     rnorm = 1.0 / jnp.sqrt(jnp.sum(emb * emb, axis=1, keepdims=True) + 1e-06)
-    unit = emb * rnorm
-    u_hi, u_lo = hi_lo(unit)
-    u_both = jnp.concatenate([u_hi, u_lo], axis=0)
-    lhs = jnp.concatenate([qmat, u_both], axis=0)
-    qw_copy = remote(qw_own, qw_in, p_send.at[1], p_recv.at[1], "head", partner)
-    uw_copy = remote(uw_own, uw_in, p_send.at[2], p_recv.at[2], "head", partner)
+    e_both = jnp.concatenate(hi_lo(emb), axis=0)
+    lhs = jnp.concatenate([qmat, e_both], axis=0)
+    qw_copy = remote(qw_own, qw_in, send, p_recv.at[1], "head", partner)
+    uw_copy = remote(uw_own, uw_in, send, p_recv.at[2], "head", partner)
 
     def project():
         proj = mm(lhs, w_half(1 - side), NT)
         qw_own[...] = proj[:nq].astype(bf16)
         qw_copy.start()
-        uw_own[...] = proj[nq:nq + docs] + proj[nq + docs:]
+        uw_own[...] = rnorm * (proj[nq:nq + docs] + proj[nq + docs:])
         uw_copy.start()
 
     pl.when(side == 1)(project)
-    sims = sim_scale * mm(u_both, qmat, NT)
-    logits = sims[:docs]
-    full = logits + sims[docs:]
+    sims = mm(e_both, qmat, NT)
+    logits = (sim_scale * rnorm) * (sims[:docs] + sims[docs:])
     top = jnp.max(logits, axis=0, keepdims=True)
     total = jnp.sum(jnp.exp(logits - top), axis=0, keepdims=True)
     hit = jnp.sum(logits * chosen, axis=0, keepdims=True)
@@ -317,20 +321,18 @@
     pl.when(side == 0)(project)
     proj = mm(lhs, w_half(side), NT)
     qw_mine = proj[:nq].astype(bf16)
-    uw = proj[nq:nq + docs] + proj[nq + docs:]
+    uw = rnorm * (proj[nq:nq + docs] + proj[nq + docs:])
     factor = rnorm * (loss_scale / len_f)
 
     c_copy.wait_recv()
-    other = jnp.concatenate(
-        [jnp.where(member, c_in[h:h + 1, :], 0.0) for h in range(heads)], axis=0
-    )
-    both = jnp.concatenate([spread, other], axis=0)
-    b_hi, b_lo = hi_lo(both)
-    a_ref[...] = jnp.concatenate([b_hi, b_lo], axis=0)
+    rows_of = [spread[h * docs:(h + 1) * docs] for h in range(heads)]
+    rows_of += [jnp.where(member, c_in[h:h + 1, :], 0.0) for h in range(heads)]
+    for part in range(2):
+        b_hi, b_lo = hi_lo(jnp.concatenate(rows_of[part::2], axis=0))
+        a_ref[part] = jnp.concatenate([b_hi, b_lo], axis=0)
 
     qw_copy.wait_recv()
     qw = jnp.concatenate([qw_mine, qw_in[...]], axis=1)
-    qw2 = jnp.concatenate([qw, qw], axis=0)
     uw_copy.wait_recv()
     uw2 = factor * jnp.concatenate([uw, uw_in[...]], axis=1)
     factor = factor * sim_scale
@@ -349,20 +351,19 @@
     total, hit = fold(n_dp, gather, (zero, zero))
     dl = shifted * (1.0 / total) - chosen
     d_hi, d_lo = hi_lo(dl)
-    g = mm(jnp.concatenate([d_hi, d_lo], axis=1), qw2, NN)
-    inner = jnp.sum(dl * full, axis=1, keepdims=True)
+    g = mm(jnp.concatenate([d_hi, d_lo], axis=0), qw, NN)
+    g = g[:docs] + g[docs:]
+    inner = jnp.sum(dl * logits, axis=1, keepdims=True)
     loss_ref[0, 0] = jnp.sum(top + jnp.log(total) - hit) * (1.0 / nq)
     g = factor * g - inner * uw2
-    small = jnp.concatenate(
-        [g[:, h * half:(h + 1) * half] for h in range(2 * heads)], axis=0
-    )
-    small = jnp.concatenate([small, small], axis=0).T.astype(bf16)
-    out_ref[...] = mm(small, a_ref[...], NN).astype(bf16)
-
-    wait_all(qall.at[pl.ds(0, peers)], q_send)
-    pl.when(head == 0)(lambda: wait_all(emb_slot.at[0], e_send))
-    pl.when(head > 0)(lambda: wait_all(emb_slot.at[pl.ds(0, n_head - 1)], e_send))
-    wait_all(stat.at[pl.ds(0, n_dp - 1)], s_send)
+    tiles = [g[:, t * HD:(t + 1) * HD] for t in range(heads)]
+    small = jnp.concatenate(tiles + tiles, axis=0).T.astype(bf16)
+    out_ref[...] = (mm(small[:half], a_ref[0], NN) + mm(small[half:], a_ref[1], NN)).astype(bf16)
+
+    wait_all(qall.at[pl.ds(0, peers)], send)
+    pl.when(head == 0)(lambda: wait_all(emb_slot.at[0], send))
+    pl.when(head > 0)(lambda: wait_all(emb_slot.at[pl.ds(0, n_head - 1)], send))
+    wait_all(stat.at[pl.ds(0, n_dp - 1)], send)
     c_copy.wait_send()
     qw_copy.wait_send()
     uw_copy.wait_send()
@@ -417,18 +418,15 @@
             pltpu.VMEM((nq, half), bf16),
             pltpu.VMEM((docs, half), f32),
             pltpu.VMEM((docs, half), f32),
-            pltpu.VMEM((4 * heads * docs, seq), bf16),
+            pltpu.VMEM((2, 2 * heads * docs, seq), bf16),
             pltpu.VMEM((docs, model), bf16),
             pltpu.SemaphoreType.REGULAR((n_head,)),
             dma((6,)),
             dma,
             dma,
             dma,
+            dma((2,)),
             dma,
-            dma((n_head,)),
-            dma,
-            dma,
-            dma((3,)),
             dma((3,)),
         ],
         compiler_params=pltpu.CompilerParams(collective_id=0, has_side_effects=True),

time: 16.4 us -> 16 us (0.976)
  Pallas kernels: 15.6 us -> 15.2 us
    pallas_call x1, Pallas kernels: 14.9 us -> 14.6 us  [per_device(): pl.pallas_call(functools.partial(kernel, n_dp, n_head), out_shape=(pltpu....]
where the time goes in v4:
time: 16 us; the launch traced here: 15.9 us
  Pallas kernels  15.2 us (95%)
  between operations  0.64 us (4%)
    pallas_call x1, Pallas kernels, per_device(): pl.pallas_call(functools.partial(kernel, n_dp, n_head), out_shape=(pltpu....  14.6 us
    pallas_call x1, Pallas kernels, per_device(): pl.pallas_call(store, out_shape=(jax.ShapeDtypeStruct((HD // 2, seq), bf1...  0.66 us

profile of v4, /device:TPU:0, one launch (start us, length us, event | category | flops | bytes accessed | tf_op | source)
XLA Modules:
  0.0 15.9 jit_solution(4155985172887922827)
XLA Ops:
  0.6 14.6 %shard_map.86 = (bf16[64,512]{1,0:T(8,128)(2,1)S(1)}, f32[1,1]{1,0:T(1,128)S(4)}) custom-call(s32[1,8]{1,0:T(1,128)} %lens_hbm.1, s32[1,32]{1,0:T(1,128)} %bitcast.3, bf16[512,384]{1,0:T(8,128)(2,1)} %q_hbm.1, bf16[512,256]{1,0:T(8,128)(2,1)} %k_hbm.1, bf16[512,256]{1,0:T(8,128)(2,1)} %v_hbm.1, bf16[384,1536]{1,0:T(8,128)(2,1)} %w_hbm.1, bf16[4,384]{1,0:T(4,128)(2,1)} %qry_hbm.1), custom_call_target="tpu_custom_call" | custom-call | tf_op jit(solution)/shard_map/pallas_call | solution.py:396
  15.2 0.7 %shard_map.87 = (bf16[64,512]{1,0:T(8,128)(2,1)}, f32[1,1]{1,0:T(1,128)}) custom-call(bf16[64,512]{1,0:T(8,128)(2,1)S(1)} %get-tuple-element.6.x_ref, f32[1,1]{1,0:T(1,128)S(4)} %get-tuple-element.7.l_ref), custom_call_target="tpu_custom_call" | custom-call | tf_op jit(solution)/shard_map/pallas_call | solution.py:436
